TPU v7x, 32 devices: a whole 2x2x4 slice. The times are simulated.
32 devices in a mesh: dp: 8 (over z, y), neg: 4 (over x, core).
Axes of the slice: x: 2, y: 2, z: 4, core: 2. Of those that a mesh axis runs over, the one named last changes fastest.
Arguments:
- user_embed: bfloat16 [24576, 256], P(('dp', 'neg')), may hold values from -25 to 25
- positive_embed: bfloat16 [24576, 256], P(('dp', 'neg')), may hold values from -6 to 6
- positive_ids: int32 [24576], P(('dp', 'neg')), may hold values from 0 to 1048575
- token_weights: int32 [24576], P(('dp', 'neg')), may hold values from 1 to 5
- offsets: int32 [8, 25], P('dp'), may hold values from 0 to 3072, as said below
- negative_embed: bfloat16 [32768, 256], P('neg'), may hold values from -6 to 6
- negative_ids: int32 [32768], P('neg'), may hold values from 0 to 1048575
Outputs:
- token_loss: float32 [24576], P(('dp', 'neg'))
- mean_loss: float32 [], replicated
Inputs may be any that keep to these rules, and one draw needn't show every extreme that they name: `offsets`: each row starts at 0 and does not fall; every user holds 2 or more slots; in every draw some group fills all 3072 slots.
All inputs are finite; a program needn't handle non-finite values.
Results may differ from a plain program's by a relative error of at most 0.0003.
Values may be sent and summed in bfloat16 or wider, within the bound.
No kernel may reach another device: no remote copies, remote signals or barrier semaphores. Data moves between devices by JAX's collectives and lax.ppermute only.
A program may use at most 64 MiB of HBM per device.

v0:
```python
import math
import jax
import jax.numpy as jnp
from jax import lax
from jax.sharding import PartitionSpec as P

floor_value = -1e30


def merged(value, axis, join):
    pieces = jax.tree.map(lambda part: lax.all_gather(part, axis), value)
    head = jax.tree.map(lambda part: part[0], pieces)
    tail = jax.tree.map(lambda part: part[1:], pieces)
    total, _ = lax.scan(lambda total, share: (join(total, share), None), head, tail)
    return total


def shard_partials(rows, row_ids, columns, column_ids, scale):
    logits = (
        lax.dot_general(rows, columns, (((1,), (1,)), ((), ())), preferred_element_type=jnp.float32)
        * scale
    )
    hit = row_ids[:, None] == column_ids[None, :]
    peak = jnp.max(jnp.where(hit, floor_value, logits), axis=1)
    summed = jnp.sum(jnp.where(hit, 0.0, jnp.exp(logits - peak[:, None])), axis=1)
    return (peak, summed)


def combine(first, second):
    peak = jnp.maximum(first[0], second[0])
    return (peak, first[1] * jnp.exp(first[0] - peak) + second[1] * jnp.exp(second[0] - peak))


def shards(
    user_embed, positive_embed, positive_ids, token_weights, offsets, negative_embed, negative_ids
):
    tok_rows = user_embed.shape[0]
    width = user_embed.shape[1]
    scale = 3.0 / math.sqrt(width)
    positions = lax.axis_index("neg") * tok_rows + jnp.arange(tok_rows, dtype=jnp.int32)
    ends = offsets[0, 1:]
    last_slot = jnp.any(positions[:, None] + 1 == ends[None, :], axis=1)
    live = (positions < offsets[0, -1]) & jnp.logical_not(last_slot)
    weight = token_weights.astype(jnp.float32)
    live_weight = weight * live.astype(jnp.float32)
    rows = lax.all_gather(user_embed, "neg", axis=0, tiled=True)
    row_ids = lax.all_gather(positive_ids, "neg", axis=0, tiled=True)
    number = rows.shape[0]
    block = math.gcd(number, 512)
    blocks = rows.reshape(number // block, block, width)
    id_blocks = row_ids.reshape(number // block, block)

    def one_block(pair):
        return shard_partials(pair[0], pair[1], negative_embed, negative_ids, scale)

    peaks, sums = lax.map(one_block, (blocks, id_blocks))
    new_peaks = peaks.reshape(number)
    new_sums = sums.reshape(number)
    peaks = new_peaks
    sums = new_sums
    peaks, sums = merged((peaks, sums), "neg", combine)
    own_start = lax.axis_index("neg") * tok_rows
    peaks = lax.dynamic_slice_in_dim(peaks, own_start, tok_rows, 0)
    sums = lax.dynamic_slice_in_dim(sums, own_start, tok_rows, 0)
    positive = (
        jnp.sum(user_embed.astype(jnp.float32) * positive_embed.astype(jnp.float32), axis=1) * scale
    )
    top = jnp.maximum(peaks, positive)
    lse = top + jnp.log(sums * jnp.exp(peaks - top) + jnp.exp(positive - top))
    token_loss = jnp.where(live, lse - positive, 0.0).astype(jnp.float32)
    weighted = jnp.sum(weight * token_loss)
    total, count = lax.psum((weighted, jnp.sum(live_weight)), ("dp", "neg"))
    return (token_loss, total / count)


def solution(mesh):
    in_specs = (
        P(("dp", "neg"), None),
        P(("dp", "neg"), None),
        P(("dp", "neg")),
        P(("dp", "neg")),
        P("dp", None),
        P("neg", None),
        P("neg"),
    )
    out_specs = (P(("dp", "neg")), P())
    return jax.shard_map(shards, mesh=mesh, in_specs=in_specs, out_specs=out_specs, check_vma=False)
```

profile of v0, /device:TPU:0, one launch (start us, length us, event | category | flops | bytes accessed | tf_op | source)
XLA Modules:
  0.0 153.4 jit_solution(13548246562837746475)
XLA Ops:
  7.2 0.0 all-gather.5.cloned.1.call-start
  7.2 0.7 all-gather.5.cloned.1.call-update
  7.9 0.7 reshape.22
  8.6 6.2 %all-gather = s32[4,1,768]{2,1,0:T(1,128)S(1)} all-gather(s32[1,1,768]{2,1,0:T(1,128)S(1)} %reshape.22), channel_id=1, replica_groups=mesh['dp'=8,'neg'=4] {'neg'}, dimensions={0}, use_global_device_ids=true | all-gather | bytes 15360 | tf_op jit(solution)/shard_map/all_gather | solution.py:47
  14.9 1.2 slice.18
  16.1 0.7 slice_bitcast_fusion
  16.8 0.1 compare_reduce_fusion
  16.9 1.3 multiply_reduce_fusion
  18.2 13.7 %all-gather.5.cloned.1.call-done = bf16[3072,256]{1,0:T(8,128)(2,1)} async-done(((bf16[768,256]{1,0:T(8,128)(2,1)}), bf16[3072,256]{1,0:T(8,128)(2,1)}) %all-gather.5.cloned.1.call-update) | async-done | bytes 1572880 | tf_op jit(solution)/shard_map/all_gather | solution.py:46
  31.9 0.0 copy-start.1
  31.9 59.9 %while.24 = (s32[]{:T(128)}, f32[6,512]{1,0:T(8,128)S(1)}, f32[6,512]{1,0:T(8,128)S(1)}, s32[6,512]{1,0:T(8,128)S(1)}, s32[8192]{0:T(1024)}, /*index=5*/bf16[6,5...) while((s32[]{:T(128)}, f32[6,512]{1,0:T(8,128)S(1)}, f32[6,512]{1,0:T(8,128)S(1)}, ...), condition=%wide.region_4.5_spmd, body=%wide.region_1.4_spmd.sunk | while | flops 2185231360 | bytes 38230660 | solution.py:56
  31.9 0.0 copy-start
  31.9 5.1 %fusion.16 = (f32[512]{0:T(512)S(1)}, f32[512,8192]{1,0:T(8,128)S(1)}) fusion(s32[8192]{0:T(1024)} %get-tuple-element.215, s32[512]{0:T(512)S(1)} %bitcast.44, bf16[8192,256]{1,0:T(8,128)(2,1)} %get-tuple-element.217, bf16[6,512,256]{2,1,0:T(8,128)(2,1)} %get-tuple-element.216, s32[]{:T(128)} %get-tuple-element.202), kind=kOutput, calls=%fused_computation.2.clone.1 | convolution fusion | flops 2164260352 | bytes 21271040 | tf_op jit(solution)/shard_map/while/body/eval_jaxpr/dot_general | solution.py:20
  37.1 0.0 copy-done
  37.1 4.6 %fusion.17 = f32[512]{0:T(512)S(1)} fusion(f32[512,8192]{1,0:T(8,128)S(1)} %get-tuple-element.183, f32[512]{0:T(512)S(1)} %get-tuple-element.182, s32[8192]{0:T(1024)S(1)} %copy-done, s32[512]{0:T(512)S(1)} %bitcast.45), kind=kLoop, calls=%fused_computation.3.clone.1 | loop fusion | flops 20971008 | bytes 16816128 | tf_op jit(solution)/shard_map/while/body/eval_jaxpr/reduce_sum | solution.py:25
  41.7 0.1 dynamic_update_slice.10
  41.8 0.1 dynamic_update_slice.9
  41.9 0.0 copy-start
  41.9 5.1 %fusion.16 = (f32[512]{0:T(512)S(1)}, f32[512,8192]{1,0:T(8,128)S(1)}) fusion(s32[8192]{0:T(1024)} %get-tuple-element.215, s32[512]{0:T(512)S(1)} %bitcast.44, bf16[8192,256]{1,0:T(8,128)(2,1)} %get-tuple-element.217, bf16[6,512,256]{2,1,0:T(8,128)(2,1)} %get-tuple-element.216, s32[]{:T(128)} %get-tuple-element.202), kind=kOutput, calls=%fused_computation.2.clone.1 | convolution fusion | flops 2164260352 | bytes 21271040 | tf_op jit(solution)/shard_map/while/body/eval_jaxpr/dot_general | solution.py:20
  47.1 0.0 copy-done
  47.1 4.6 %fusion.17 = f32[512]{0:T(512)S(1)} fusion(f32[512,8192]{1,0:T(8,128)S(1)} %get-tuple-element.183, f32[512]{0:T(512)S(1)} %get-tuple-element.182, s32[8192]{0:T(1024)S(1)} %copy-done, s32[512]{0:T(512)S(1)} %bitcast.45), kind=kLoop, calls=%fused_computation.3.clone.1 | loop fusion | flops 20971008 | bytes 16816128 | tf_op jit(solution)/shard_map/while/body/eval_jaxpr/reduce_sum | solution.py:25
  51.7 0.1 dynamic_update_slice.10
  51.8 0.1 dynamic_update_slice.9
  51.9 0.0 copy-start
  51.9 5.1 %fusion.16 = (f32[512]{0:T(512)S(1)}, f32[512,8192]{1,0:T(8,128)S(1)}) fusion(s32[8192]{0:T(1024)} %get-tuple-element.215, s32[512]{0:T(512)S(1)} %bitcast.44, bf16[8192,256]{1,0:T(8,128)(2,1)} %get-tuple-element.217, bf16[6,512,256]{2,1,0:T(8,128)(2,1)} %get-tuple-element.216, s32[]{:T(128)} %get-tuple-element.202), kind=kOutput, calls=%fused_computation.2.clone.1 | convolution fusion | flops 2164260352 | bytes 21271040 | tf_op jit(solution)/shard_map/while/body/eval_jaxpr/dot_general | solution.py:20
  57.1 0.0 copy-done
  57.1 4.6 %fusion.17 = f32[512]{0:T(512)S(1)} fusion(f32[512,8192]{1,0:T(8,128)S(1)} %get-tuple-element.183, f32[512]{0:T(512)S(1)} %get-tuple-element.182, s32[8192]{0:T(1024)S(1)} %copy-done, s32[512]{0:T(512)S(1)} %bitcast.45), kind=kLoop, calls=%fused_computation.3.clone.1 | loop fusion | flops 20971008 | bytes 16816128 | tf_op jit(solution)/shard_map/while/body/eval_jaxpr/reduce_sum | solution.py:25
  61.7 0.1 dynamic_update_slice.10
  61.8 0.1 dynamic_update_slice.9
  61.9 0.0 copy-start
  61.9 5.1 %fusion.16 = (f32[512]{0:T(512)S(1)}, f32[512,8192]{1,0:T(8,128)S(1)}) fusion(s32[8192]{0:T(1024)} %get-tuple-element.215, s32[512]{0:T(512)S(1)} %bitcast.44, bf16[8192,256]{1,0:T(8,128)(2,1)} %get-tuple-element.217, bf16[6,512,256]{2,1,0:T(8,128)(2,1)} %get-tuple-element.216, s32[]{:T(128)} %get-tuple-element.202), kind=kOutput, calls=%fused_computation.2.clone.1 | convolution fusion | flops 2164260352 | bytes 21271040 | tf_op jit(solution)/shard_map/while/body/eval_jaxpr/dot_general | solution.py:20
  67.0 0.0 copy-done
  67.1 4.6 %fusion.17 = f32[512]{0:T(512)S(1)} fusion(f32[512,8192]{1,0:T(8,128)S(1)} %get-tuple-element.183, f32[512]{0:T(512)S(1)} %get-tuple-element.182, s32[8192]{0:T(1024)S(1)} %copy-done, s32[512]{0:T(512)S(1)} %bitcast.45), kind=kLoop, calls=%fused_computation.3.clone.1 | loop fusion | flops 20971008 | bytes 16816128 | tf_op jit(solution)/shard_map/while/body/eval_jaxpr/reduce_sum | solution.py:25
  71.7 0.1 dynamic_update_slice.10
  71.8 0.1 dynamic_update_slice.9
  71.9 0.0 copy-start
  71.9 5.1 %fusion.16 = (f32[512]{0:T(512)S(1)}, f32[512,8192]{1,0:T(8,128)S(1)}) fusion(s32[8192]{0:T(1024)} %get-tuple-element.215, s32[512]{0:T(512)S(1)} %bitcast.44, bf16[8192,256]{1,0:T(8,128)(2,1)} %get-tuple-element.217, bf16[6,512,256]{2,1,0:T(8,128)(2,1)} %get-tuple-element.216, s32[]{:T(128)} %get-tuple-element.202), kind=kOutput, calls=%fused_computation.2.clone.1 | convolution fusion | flops 2164260352 | bytes 21271040 | tf_op jit(solution)/shard_map/while/body/eval_jaxpr/dot_general | solution.py:20
  77.0 0.0 copy-done
  77.0 4.6 %fusion.17 = f32[512]{0:T(512)S(1)} fusion(f32[512,8192]{1,0:T(8,128)S(1)} %get-tuple-element.183, f32[512]{0:T(512)S(1)} %get-tuple-element.182, s32[8192]{0:T(1024)S(1)} %copy-done, s32[512]{0:T(512)S(1)} %bitcast.45), kind=kLoop, calls=%fused_computation.3.clone.1 | loop fusion | flops 20971008 | bytes 16816128 | tf_op jit(solution)/shard_map/while/body/eval_jaxpr/reduce_sum | solution.py:25
  81.7 0.1 dynamic_update_slice.10
  81.8 0.1 dynamic_update_slice.9
  81.8 0.0 copy-start
  81.9 5.1 %fusion.16 = (f32[512]{0:T(512)S(1)}, f32[512,8192]{1,0:T(8,128)S(1)}) fusion(s32[8192]{0:T(1024)} %get-tuple-element.215, s32[512]{0:T(512)S(1)} %bitcast.44, bf16[8192,256]{1,0:T(8,128)(2,1)} %get-tuple-element.217, bf16[6,512,256]{2,1,0:T(8,128)(2,1)} %get-tuple-element.216, s32[]{:T(128)} %get-tuple-element.202), kind=kOutput, calls=%fused_computation.2.clone.1 | convolution fusion | flops 2164260352 | bytes 21271040 | tf_op jit(solution)/shard_map/while/body/eval_jaxpr/dot_general | solution.py:20
  87.0 0.0 copy-done
  87.0 4.6 %fusion.17 = f32[512]{0:T(512)S(1)} fusion(f32[512,8192]{1,0:T(8,128)S(1)} %get-tuple-element.183, f32[512]{0:T(512)S(1)} %get-tuple-element.182, s32[8192]{0:T(1024)S(1)} %copy-done, s32[512]{0:T(512)S(1)} %bitcast.45), kind=kLoop, calls=%fused_computation.3.clone.1 | loop fusion | flops 20971008 | bytes 16816128 | tf_op jit(solution)/shard_map/while/body/eval_jaxpr/reduce_sum | solution.py:25
  91.7 0.1 dynamic_update_slice.10
  91.7 0.1 dynamic_update_slice.9
  91.8 5.2 %all-gather.2 = f32[4,1,3072]{2,1,0:T(1,128)S(1)} all-gather(f32[1,1,3072]{2,1,0:T(1,128)S(1)} %reshape.26), channel_id=1, replica_groups=mesh['dp'=8,'neg'=4] {'neg'}, dimensions={0}, use_global_device_ids=true | all-gather | bytes 61440 | tf_op jit(solution)/shard_map/all_gather | solution.py:11
  97.1 5.2 %all-gather.1 = f32[4,1,3072]{2,1,0:T(1,128)S(1)} all-gather(f32[1,1,3072]{2,1,0:T(1,128)S(1)} %reshape.24), channel_id=1, replica_groups=mesh['dp'=8,'neg'=4] {'neg'}, dimensions={0}, use_global_device_ids=true | all-gather | bytes 61440 | tf_op jit(solution)/shard_map/all_gather | solution.py:11
  102.4 0.2 while.25
  102.6 0.0 copy-done.1
  102.6 2.0 %select_reduce_fusion = (f32[]{:T(128)}, f32[]{:T(128)}, f32[768]{0:T(1024)}) fusion(s32[768]{0:T(1024)S(1)} %copy-done.1, pred[768]{0:T(1024)(128)(4,1)S(1)} %compare_reduce_fusion, s32[]{:T(128)} %bitcast.6, s32[]{:T(128)S(6)} %mul.31, f32[3072]{0:T(1024)S(1)} %get-tuple-element.71, s32[]{:T(128)S(6)} %select_n.15, f32[768]{0:T(1024)S(1)} %multiply_reduce_fusion, ...), kind=kLoop, calls=%fused_computation.16 | loop fusion | flops 13822 | bytes 16148 | tf_op jit(solution)/shard_map/reduce_sum | solution.py:72
  104.6 39.5 %all-reduce = (f32[]{:T(128)}, f32[]{:T(128)}) all-reduce(f32[]{:T(128)} %get-tuple-element.73, f32[]{:T(128)} %get-tuple-element.72), channel_id=1, replica_groups=mesh['dp'=8,'neg'=4] {'dp','neg'}, use_global_device_ids=true, to_apply=%region_9.10 | all-reduce | flops 2 | bytes 16 | tf_op jit(solution)/shard_map/psum | solution.py:72
  (25 shorter events, 0.3 us)
Async XLA Ops:
  7.2 24.8 %all-gather.5.cloned.1.call-start = ((), (), s32[]{:S(2)}) async-start(), calls=%async_computation | async-start | bytes 1966080 | tf_op jit(solution)/shard_map/all_gather | solution.py:46
  31.9 70.7 %copy-start.1 = (s32[768]{0:T(1024)S(1)}, s32[768]{0:T(1024)}, u32[]{:S(2)}) copy-start(s32[768]{0:T(1024)} %param.14) | copy-start | bytes 9220
  31.9 5.2 %copy-start = (s32[8192]{0:T(1024)S(1)}, s32[8192]{0:T(1024)}, u32[]{:S(2)}) copy-start(s32[8192]{0:T(1024)} %get-tuple-element.215) | copy-start | bytes 98308 | tf_op jit(solution)/shard_map/while
  41.9 5.2 %copy-start = (s32[8192]{0:T(1024)S(1)}, s32[8192]{0:T(1024)}, u32[]{:S(2)}) copy-start(s32[8192]{0:T(1024)} %get-tuple-element.215) | copy-start | bytes 98308 | tf_op jit(solution)/shard_map/while
  51.9 5.2 %copy-start = (s32[8192]{0:T(1024)S(1)}, s32[8192]{0:T(1024)}, u32[]{:S(2)}) copy-start(s32[8192]{0:T(1024)} %get-tuple-element.215) | copy-start | bytes 98308 | tf_op jit(solution)/shard_map/while
  61.9 5.2 %copy-start = (s32[8192]{0:T(1024)S(1)}, s32[8192]{0:T(1024)}, u32[]{:S(2)}) copy-start(s32[8192]{0:T(1024)} %get-tuple-element.215) | copy-start | bytes 98308 | tf_op jit(solution)/shard_map/while
  71.9 5.2 %copy-start = (s32[8192]{0:T(1024)S(1)}, s32[8192]{0:T(1024)}, u32[]{:S(2)}) copy-start(s32[8192]{0:T(1024)} %get-tuple-element.215) | copy-start | bytes 98308 | tf_op jit(solution)/shard_map/while
  81.8 5.2 %copy-start = (s32[8192]{0:T(1024)S(1)}, s32[8192]{0:T(1024)}, u32[]{:S(2)}) copy-start(s32[8192]{0:T(1024)} %get-tuple-element.215) | copy-start | bytes 98308 | tf_op jit(solution)/shard_map/while
Sparse Core Ops, SparseCore 0:
  9.5 22.3 all-gather.4
where the time goes:
time: 154 us; the launch traced here: 153 us
  blocking collectives  56.2 us (36%)
  other arithmetic  31.4 us (20%)
  matrix products  30.9 us (20%)
  between operations  16.6 us (11%)
  waiting for transfers between devices  14.4 us (9%)
  local copies, waits for them, and re-layouts  3.64 us (2%)
    psum x1, blocking collectives, shards(): total, count = lax.psum((weighted, jnp.sum(live_weight)), ('dp', 'neg'))  39.5 us
    dot_general x6, matrix products, shard_partials(): lax.dot_general(rows, columns, (((1,), (1,)), ((), ())), preferred_elemen...  30.9 us
    reduce_sum x6, other arithmetic, shard_partials(): jnp.sum(jnp.where(hit, 0.0, jnp.exp(logits - peak[:, None])), axis=1)  27.9 us
    all_gather x1, waiting for transfers between devices, shards(): rows = lax.all_gather(user_embed, 'neg', axis=0, tiled=True)  13.7 us
    all_gather x2, blocking collectives, merged(): pieces = jax.tree.map(lambda part: lax.all_gather(part, axis), value)  10.4 us
    all_gather x1, blocking collectives, shards(): row_ids = lax.all_gather(positive_ids, 'neg', axis=0, tiled=True)  6.2 us
  transfers between devices with their start and end apart: 1, of which 1 were waited for; matrix products, arithmetic and copies ran while one was open for 3% of the time, Pallas kernels for 0%

commit v1 on v0

--- a/solution.py
+++ b/solution.py
@@ -43,7 +43,12 @@
     live = (positions < offsets[0, -1]) & jnp.logical_not(last_slot)
     weight = token_weights.astype(jnp.float32)
     live_weight = weight * live.astype(jnp.float32)
-    rows = lax.all_gather(user_embed, "neg", axis=0, tiled=True)
+    ring = [user_embed]
+    for hop in range(3):
+        ring.append(lax.ppermute(ring[-1], "neg", [(dev, (dev + 1) % 4) for dev in range(4)]))
+    rows = jnp.roll(
+        jnp.concatenate(ring[::-1], axis=0), (lax.axis_index("neg") + 1) * ring[0].shape[0], axis=0
+    )
     row_ids = lax.all_gather(positive_ids, "neg", axis=0, tiled=True)
     number = rows.shape[0]
     block = math.gcd(number, 512)

time: 154 us -> 140 us (0.909)
  between operations: 16.6 us -> 3.25 us
  matrix products: 30.9 us -> 29.3 us
    ppermute x0 -> x3, waiting for transfers between devices: none -> 14.8 us  [shards(): lax.ppermute(ring[-1], 'neg', [(dev, (dev + 1) % 4) for dev in range(4)])]
    all_gather x1 -> x0, waiting for transfers between devices: 13.7 us -> none  [shards(): rows = lax.all_gather(user_embed, 'neg', axis=0, tiled=True)]
    dot_general x6, matrix products: 30.9 us -> 29.3 us  [shard_partials(): lax.dot_general(rows, columns, (((1,), (1,)), ((), ())), preferred_elemen...]
  transfers between devices with their start and end apart: 1 -> 3, of which waited for: 1 -> 2; matrix products, arithmetic and copies ran while one was open for 3% -> 3% of each run, Pallas kernels for 0% -> 0%
where the time goes in v1:
time: 140 us
  blocking collectives  57.3 us (41%)
  other arithmetic  30 us (21%)
  matrix products  29.3 us (21%)
  waiting for transfers between devices  14.8 us (11%)
  local copies, waits for them, and re-layouts  4.43 us (3%)
  between operations  3.25 us (2%)
    psum x1, blocking collectives, shards(): total, count = lax.psum((weighted, jnp.sum(live_weight)), ('dp', 'neg'))  40.6 us
    dot_general x6, matrix products, shard_partials(): lax.dot_general(rows, columns, (((1,), (1,)), ((), ())), preferred_elemen...  29.3 us
    reduce_sum x6, other arithmetic, shard_partials(): jnp.sum(jnp.where(hit, 0.0, jnp.exp(logits - peak[:, None])), axis=1)  26.5 us
    ppermute x3, waiting for transfers between devices, shards(): lax.ppermute(ring[-1], 'neg', [(dev, (dev + 1) % 4) for dev in range(4)])  14.8 us
    all_gather x2, blocking collectives, merged(): pieces = jax.tree.map(lambda part: lax.all_gather(part, axis), value)  10.4 us
    all_gather x1, blocking collectives, shards(): row_ids = lax.all_gather(positive_ids, 'neg', axis=0, tiled=True)  6.25 us
  transfers between devices with their start and end apart: 3, of which 2 were waited for; matrix products, arithmetic and copies ran while one was open for 3% of the time, Pallas kernels for 0%

profile of v1, /device:TPU:0, one launch (start us, length us, event | category | flops | bytes accessed | tf_op | source)
XLA Modules:
  0.0 140.0 jit_solution(13950672036128355245)
XLA Ops:
  0.6 0.0 copy-start
  0.6 0.5 collective-permute-start
  1.2 7.6 %collective-permute-done = bf16[768,256]{1,0:T(8,128)(2,1)S(1)} collective-permute-done((bf16[768,256]{1,0:T(8,128)(2,1)}, bf16[768,256]{1,0:T(8,128)(2,1)S(1)}, u32[]{:S(2)}, u32[]{:S(2)}) %collective-permute-start) | collective-permute-done | bytes 393248 | tf_op jit(solution)/shard_map/ppermute | solution.py:48
  8.8 0.0 collective-permute-start.1
  8.8 7.2 %collective-permute-done.1 = bf16[768,256]{1,0:T(8,128)(2,1)S(1)} collective-permute-done((bf16[768,256]{1,0:T(8,128)(2,1)S(1)}, bf16[768,256]{1,0:T(8,128)(2,1)S(1)}, u32[]{:S(2)}, u32[]{:S(2)}) %collective-permute-start.1) | collective-permute-done | bytes 393248 | tf_op jit(solution)/shard_map/ppermute | solution.py:48
  16.0 0.0 collective-permute-start.2
  16.0 0.7 slice_bitcast_fusion
  16.7 1.2 slice.18
  18.0 0.7 reshape.22
  18.6 6.3 %all-gather = s32[4,1,768]{2,1,0:T(1,128)S(1)} all-gather(s32[1,1,768]{2,1,0:T(1,128)S(1)} %reshape.22), channel_id=1, replica_groups=mesh['dp'=8,'neg'=4] {'neg'}, dimensions={0}, use_global_device_ids=true | all-gather | bytes 15360 | tf_op jit(solution)/shard_map/all_gather | solution.py:52
  25.0 0.1 compare_reduce_fusion
  25.1 1.3 multiply_reduce_fusion
  26.4 0.0 collective-permute-done.2
  26.5 0.0 copy-done
  26.5 0.0 copy-start.1
  26.7 0.4 constant_dynamic-slice_fusion.3
  27.1 0.2 copy-done.1
  27.3 0.0 copy-start.2
  27.3 56.9 %while.24 = (s32[]{:T(128)}, f32[6,512]{1,0:T(8,128)S(1)}, f32[6,512]{1,0:T(8,128)S(1)}, s32[6,512]{1,0:T(8,128)S(1)}, s32[8192]{0:T(1024)S(1)}, /*index=5*/bf16...) while((s32[]{:T(128)}, f32[6,512]{1,0:T(8,128)S(1)}, f32[6,512]{1,0:T(8,128)S(1)}, ...), condition=%wide.region_4.5_spmd, body=%wide.region_1.4_spmd.sunk | while | flops 2185231360 | bytes 38099052 | solution.py:61
  27.3 4.9 %fusion.16 = (f32[512]{0:T(512)S(1)}, f32[512,8192]{1,0:T(8,128)S(1)}) fusion(s32[8192]{0:T(1024)S(1)} %get-tuple-element.215, s32[512]{0:T(512)S(1)} %bitcast.45, bf16[8192,256]{1,0:T(8,128)(2,1)} %get-tuple-element.217, bf16[6,512,256]{2,1,0:T(8,128)(2,1)S(1)} %get-tuple-element.216, s32[]{:T(128)} %get-tuple-element.202), kind=kOutput, calls=%fused_computation.2.clone.1 | convolution fusion | flops 2164260352 | bytes 21270532 | tf_op jit(solution)/shard_map/while/body/eval_jaxpr/dot_general | solution.py:20
  32.2 4.4 %fusion.17 = f32[512]{0:T(512)S(1)} fusion(f32[512,8192]{1,0:T(8,128)S(1)} %get-tuple-element.183, f32[512]{0:T(512)S(1)} %get-tuple-element.182, s32[8192]{0:T(1024)S(1)} %get-tuple-element.215, s32[512]{0:T(512)S(1)} %bitcast.46), kind=kLoop, calls=%fused_computation.3.clone.1 | loop fusion | flops 20971008 | bytes 16816128 | tf_op jit(solution)/shard_map/while/body/eval_jaxpr/reduce_sum | solution.py:25
  36.6 0.1 dynamic_update_slice.10
  36.7 0.1 dynamic_update_slice.9
  36.8 4.9 %fusion.16 = (f32[512]{0:T(512)S(1)}, f32[512,8192]{1,0:T(8,128)S(1)}) fusion(s32[8192]{0:T(1024)S(1)} %get-tuple-element.215, s32[512]{0:T(512)S(1)} %bitcast.45, bf16[8192,256]{1,0:T(8,128)(2,1)} %get-tuple-element.217, bf16[6,512,256]{2,1,0:T(8,128)(2,1)S(1)} %get-tuple-element.216, s32[]{:T(128)} %get-tuple-element.202), kind=kOutput, calls=%fused_computation.2.clone.1 | convolution fusion | flops 2164260352 | bytes 21270532 | tf_op jit(solution)/shard_map/while/body/eval_jaxpr/dot_general | solution.py:20
  41.7 4.4 %fusion.17 = f32[512]{0:T(512)S(1)} fusion(f32[512,8192]{1,0:T(8,128)S(1)} %get-tuple-element.183, f32[512]{0:T(512)S(1)} %get-tuple-element.182, s32[8192]{0:T(1024)S(1)} %get-tuple-element.215, s32[512]{0:T(512)S(1)} %bitcast.46), kind=kLoop, calls=%fused_computation.3.clone.1 | loop fusion | flops 20971008 | bytes 16816128 | tf_op jit(solution)/shard_map/while/body/eval_jaxpr/reduce_sum | solution.py:25
  46.1 0.1 dynamic_update_slice.10
  46.2 0.1 dynamic_update_slice.9
  46.3 4.9 %fusion.16 = (f32[512]{0:T(512)S(1)}, f32[512,8192]{1,0:T(8,128)S(1)}) fusion(s32[8192]{0:T(1024)S(1)} %get-tuple-element.215, s32[512]{0:T(512)S(1)} %bitcast.45, bf16[8192,256]{1,0:T(8,128)(2,1)} %get-tuple-element.217, bf16[6,512,256]{2,1,0:T(8,128)(2,1)S(1)} %get-tuple-element.216, s32[]{:T(128)} %get-tuple-element.202), kind=kOutput, calls=%fused_computation.2.clone.1 | convolution fusion | flops 2164260352 | bytes 21270532 | tf_op jit(solution)/shard_map/while/body/eval_jaxpr/dot_general | solution.py:20
  51.1 4.4 %fusion.17 = f32[512]{0:T(512)S(1)} fusion(f32[512,8192]{1,0:T(8,128)S(1)} %get-tuple-element.183, f32[512]{0:T(512)S(1)} %get-tuple-element.182, s32[8192]{0:T(1024)S(1)} %get-tuple-element.215, s32[512]{0:T(512)S(1)} %bitcast.46), kind=kLoop, calls=%fused_computation.3.clone.1 | loop fusion | flops 20971008 | bytes 16816128 | tf_op jit(solution)/shard_map/while/body/eval_jaxpr/reduce_sum | solution.py:25
  55.6 0.1 dynamic_update_slice.10
  55.6 0.1 dynamic_update_slice.9
  55.7 4.9 %fusion.16 = (f32[512]{0:T(512)S(1)}, f32[512,8192]{1,0:T(8,128)S(1)}) fusion(s32[8192]{0:T(1024)S(1)} %get-tuple-element.215, s32[512]{0:T(512)S(1)} %bitcast.45, bf16[8192,256]{1,0:T(8,128)(2,1)} %get-tuple-element.217, bf16[6,512,256]{2,1,0:T(8,128)(2,1)S(1)} %get-tuple-element.216, s32[]{:T(128)} %get-tuple-element.202), kind=kOutput, calls=%fused_computation.2.clone.1 | convolution fusion | flops 2164260352 | bytes 21270532 | tf_op jit(solution)/shard_map/while/body/eval_jaxpr/dot_general | solution.py:20
  60.6 4.4 %fusion.17 = f32[512]{0:T(512)S(1)} fusion(f32[512,8192]{1,0:T(8,128)S(1)} %get-tuple-element.183, f32[512]{0:T(512)S(1)} %get-tuple-element.182, s32[8192]{0:T(1024)S(1)} %get-tuple-element.215, s32[512]{0:T(512)S(1)} %bitcast.46), kind=kLoop, calls=%fused_computation.3.clone.1 | loop fusion | flops 20971008 | bytes 16816128 | tf_op jit(solution)/shard_map/while/body/eval_jaxpr/reduce_sum | solution.py:25
  65.0 0.1 dynamic_update_slice.10
  65.1 0.1 dynamic_update_slice.9
  65.2 4.9 %fusion.16 = (f32[512]{0:T(512)S(1)}, f32[512,8192]{1,0:T(8,128)S(1)}) fusion(s32[8192]{0:T(1024)S(1)} %get-tuple-element.215, s32[512]{0:T(512)S(1)} %bitcast.45, bf16[8192,256]{1,0:T(8,128)(2,1)} %get-tuple-element.217, bf16[6,512,256]{2,1,0:T(8,128)(2,1)S(1)} %get-tuple-element.216, s32[]{:T(128)} %get-tuple-element.202), kind=kOutput, calls=%fused_computation.2.clone.1 | convolution fusion | flops 2164260352 | bytes 21270532 | tf_op jit(solution)/shard_map/while/body/eval_jaxpr/dot_general | solution.py:20
  70.1 4.4 %fusion.17 = f32[512]{0:T(512)S(1)} fusion(f32[512,8192]{1,0:T(8,128)S(1)} %get-tuple-element.183, f32[512]{0:T(512)S(1)} %get-tuple-element.182, s32[8192]{0:T(1024)S(1)} %get-tuple-element.215, s32[512]{0:T(512)S(1)} %bitcast.46), kind=kLoop, calls=%fused_computation.3.clone.1 | loop fusion | flops 20971008 | bytes 16816128 | tf_op jit(solution)/shard_map/while/body/eval_jaxpr/reduce_sum | solution.py:25
  74.5 0.1 dynamic_update_slice.10
  74.6 0.1 dynamic_update_slice.9
  74.7 4.9 %fusion.16 = (f32[512]{0:T(512)S(1)}, f32[512,8192]{1,0:T(8,128)S(1)}) fusion(s32[8192]{0:T(1024)S(1)} %get-tuple-element.215, s32[512]{0:T(512)S(1)} %bitcast.45, bf16[8192,256]{1,0:T(8,128)(2,1)} %get-tuple-element.217, bf16[6,512,256]{2,1,0:T(8,128)(2,1)S(1)} %get-tuple-element.216, s32[]{:T(128)} %get-tuple-element.202), kind=kOutput, calls=%fused_computation.2.clone.1 | convolution fusion | flops 2164260352 | bytes 21270532 | tf_op jit(solution)/shard_map/while/body/eval_jaxpr/dot_general | solution.py:20
  79.6 4.4 %fusion.17 = f32[512]{0:T(512)S(1)} fusion(f32[512,8192]{1,0:T(8,128)S(1)} %get-tuple-element.183, f32[512]{0:T(512)S(1)} %get-tuple-element.182, s32[8192]{0:T(1024)S(1)} %get-tuple-element.215, s32[512]{0:T(512)S(1)} %bitcast.46), kind=kLoop, calls=%fused_computation.3.clone.1 | loop fusion | flops 20971008 | bytes 16816128 | tf_op jit(solution)/shard_map/while/body/eval_jaxpr/reduce_sum | solution.py:25
  84.0 0.1 dynamic_update_slice.10
  84.1 0.1 dynamic_update_slice.9
  84.2 5.2 %all-gather.2 = f32[4,1,3072]{2,1,0:T(1,128)S(1)} all-gather(f32[1,1,3072]{2,1,0:T(1,128)S(1)} %reshape.26), channel_id=1, replica_groups=mesh['dp'=8,'neg'=4] {'neg'}, dimensions={0}, use_global_device_ids=true | all-gather | bytes 61440 | tf_op jit(solution)/shard_map/all_gather | solution.py:11
  89.4 5.2 %all-gather.1 = f32[4,1,3072]{2,1,0:T(1,128)S(1)} all-gather(f32[1,1,3072]{2,1,0:T(1,128)S(1)} %reshape.24), channel_id=1, replica_groups=mesh['dp'=8,'neg'=4] {'neg'}, dimensions={0}, use_global_device_ids=true | all-gather | bytes 61440 | tf_op jit(solution)/shard_map/all_gather | solution.py:11
  94.7 0.2 while.25
  94.9 0.0 copy-done.2
  94.9 2.0 %select_reduce_fusion = (f32[]{:T(128)}, f32[]{:T(128)}, f32[768]{0:T(1024)}) fusion(s32[768]{0:T(1024)S(1)} %copy-done.2, pred[768]{0:T(1024)(128)(4,1)S(1)} %compare_reduce_fusion, s32[]{:T(128)} %bitcast.6, s32[]{:T(128)S(6)} %mul.34, f32[3072]{0:T(1024)S(1)} %get-tuple-element.71, s32[]{:T(128)S(6)} %select_n.30, f32[768]{0:T(1024)S(1)} %multiply_reduce_fusion, ...), kind=kLoop, calls=%fused_computation.24 | loop fusion | flops 13822 | bytes 16148 | tf_op jit(solution)/shard_map/reduce_sum | solution.py:77
  96.9 40.6 %all-reduce = (f32[]{:T(128)}, f32[]{:T(128)}) all-reduce(f32[]{:T(128)} %get-tuple-element.73, f32[]{:T(128)} %get-tuple-element.72), channel_id=1, replica_groups=mesh['dp'=8,'neg'=4] {'dp','neg'}, use_global_device_ids=true, to_apply=%region_9.10 | all-reduce | flops 2 | bytes 16 | tf_op jit(solution)/shard_map/psum | solution.py:77
  (33 shorter events, 0.5 us)
Async XLA Ops:
  0.6 25.9 %copy-start = (bf16[768,256]{1,0:T(8,128)(2,1)S(1)}, bf16[768,256]{1,0:T(8,128)(2,1)}, u32[]{:S(2)}) copy-start(bf16[768,256]{1,0:T(8,128)(2,1)} %param.11) | copy-start | bytes 1179652
  0.6 8.1 %collective-permute-start = (bf16[768,256]{1,0:T(8,128)(2,1)}, bf16[768,256]{1,0:T(8,128)(2,1)S(1)}, u32[]{:S(2)}, u32[]{:S(2)}) collective-permute-start(bf16[768,256]{1,0:T(8,128)(2,1)} %param.11), channel_id=1, source_target_pairs={{0,1},{1,2},{2,3},{3,0},{4,5},{5,6},{6,7},{7,4},{8,9},{9,10},{10,1... | collective-permute-start | bytes 1179656 | tf_op jit(solution)/shard_map/ppermute | solution.py:48
  8.8 7.2 %collective-permute-start.1 = (bf16[768,256]{1,0:T(8,128)(2,1)S(1)}, bf16[768,256]{1,0:T(8,128)(2,1)S(1)}, u32[]{:S(2)}, u32[]{:S(2)}) collective-permute-start(bf16[768,256]{1,0:T(8,128)(2,1)S(1)} %collective-permute-done), channel_id=1, source_target_pairs={{0,1},{1,2},{2,3},{3,0},{4,5},{5,6},{6,7},{7,4},{8,9},{9,10},{10,1... | collective-permute-start | bytes 1179656 | tf_op jit(solution)/shard_map/ppermute | solution.py:48
  16.0 10.4 %collective-permute-start.2 = (bf16[768,256]{1,0:T(8,128)(2,1)S(1)}, bf16[768,256]{1,0:T(8,128)(2,1)S(1)}, u32[]{:S(2)}, u32[]{:S(2)}) collective-permute-start(bf16[768,256]{1,0:T(8,128)(2,1)S(1)} %collective-permute-done.1), channel_id=1, source_target_pairs={{0,1},{1,2},{2,3},{3,0},{4,5},{5,6},{6,7},{7,4},{8,9},{9,10},{10,1... | collective-permute-start | bytes 1179656 | tf_op jit(solution)/shard_map/ppermute | solution.py:48
  26.5 0.8 copy-start.1
  27.3 67.6 %copy-start.2 = (s32[768]{0:T(1024)S(1)}, s32[768]{0:T(1024)}, u32[]{:S(2)}) copy-start(s32[768]{0:T(1024)} %param.14) | copy-start | bytes 9220
